TPU v7x, 32 devices: a whole 2x2x4 slice. The times are simulated.
32 devices in a mesh: wave: 8 (over z, y), lev: 4 (over x, core).
Axes of the slice: x: 2, y: 2, z: 4, core: 2. Of those that a mesh axis runs over, the one named last changes fastest.
Arguments:
- spectral: bfloat16 [32, 6, 64, 1280], P('wave', None, 'lev'), may hold values from -0.01171875 to 0.01171875
- legendre: bfloat16 [32, 640, 1280], P('wave'), may hold values from -4 to 4
- wave_ids: int32 [32], replicated, may hold values from 0 to 1279, as said below
- trunc_lengths: int32 [32], replicated, may hold values from 1 to 1280, as said below
- cycle_points: int32 [1280], replicated, may hold values from 20 to 2560, as said below
- grid_coef: float32 [1280, 2560], P('wave'), may hold values from -6 to 6
- cycle_weights: float32 [640], replicated, may hold values from 0.1 to 2
- modes_in: bfloat16 [64, 64], replicated, may hold values from -0.75 to 0.75
- modes_out: bfloat16 [64, 64], replicated, may hold values from -0.75 to 0.75
- depths: float32 [64], replicated, may hold values from 0.05 to 20
Outputs:
- update: bfloat16 [32, 6, 64, 1280], P('wave', None, 'lev')
Inputs may be any that keep to these rules, and one draw needn't show every extreme that they name: `wave_ids`: distinct zonal wavenumbers; one slot holds wavenumber 0. `trunc_lengths`: the length of slot m is at most 1280 minus wave_ids[m] and at least half of that; the slot of wavenumber 0 has length 1280. `cycle_points`: multiples of 4; cycle j and cycle 1280 - 1-j have the same count; cycles near the equator have 2560.
All inputs are finite; a program needn't handle non-finite values.
Results may differ from a plain program's by a relative error of at most 0.011.
Values may be sent and summed in bfloat16 or wider, within the bound.
A program may use at most 128 MiB of HBM per device.

v0:
```python
import jax
import jax.numpy as jnp
from jax import lax
from jax.sharding import PartitionSpec as P

NT = 1280


def trig_rows(wave_ids, cycle_count, lon_max):
    low_len = 64
    high_len = lon_max // low_len
    counts = cycle_count[:, None, None]
    count_float = counts.astype(jnp.float32)
    low_pts = jnp.arange(low_len, dtype=jnp.int32)
    high_pts = jnp.arange(high_len, dtype=jnp.int32) * low_len
    low_phase = wave_ids[None, :, None] * low_pts[None, None, :] % counts
    high_phase = wave_ids[None, :, None] * high_pts[None, None, :] % counts
    low_angle = 2.0 * jnp.pi * low_phase.astype(jnp.float32) / count_float
    high_angle = 2.0 * jnp.pi * high_phase.astype(jnp.float32) / count_float
    cos_low = jnp.cos(low_angle)[:, :, None, :]
    sin_low = jnp.sin(low_angle)[:, :, None, :]
    cos_high = jnp.cos(high_angle)[:, :, :, None]
    sin_high = jnp.sin(high_angle)[:, :, :, None]
    group_size, wave_total = (cycle_count.shape[0], wave_ids.shape[0])
    cosine = (cos_high * cos_low - sin_high * sin_low).reshape(group_size, wave_total, lon_max)
    sine = (sin_high * cos_low + cos_high * sin_low).reshape(group_size, wave_total, lon_max)
    longitude = jnp.arange(lon_max, dtype=jnp.int32)
    live_mask = (longitude[None, None, :] < counts) & (2 * wave_ids[None, :, None] < counts)
    cosine = jnp.where(live_mask, cosine, 0.0)
    sine_part = jnp.where(live_mask, -sine, 0.0)
    return jnp.stack([cosine, sine_part], axis=1).astype(jnp.bfloat16)


def cycle_trip(fourier, wave_ids, cycle_count, coef_rows):
    wave_total, channels, items, group_size = fourier.shape
    fields = channels // 2
    polys = trig_rows(wave_ids, cycle_count, coef_rows.shape[1])
    factor = jnp.where(wave_ids == 0, 1.0, 2.0).astype(jnp.bfloat16)
    weighted = (fourier * factor[:, None, None, None]).reshape(
        wave_total, 2, fields, items, group_size
    )
    grid_vals = jnp.einsum("mrfig,grmk->gfik", weighted, polys, preferred_element_type=jnp.float32)
    tendency = (grid_vals * (coef_rows[:, None, None, :] + jnp.roll(grid_vals, -1, axis=1))).astype(
        jnp.bfloat16
    )
    analysed = jnp.einsum("gfik,grmk->mrfig", tendency, polys, preferred_element_type=jnp.float32)
    analysed = analysed / cycle_count.astype(jnp.float32)
    return analysed.astype(jnp.bfloat16).reshape(wave_total, channels, items, group_size)


def cycle_group_size():
    for candidate in (8, 4, 2):
        return candidate
    return 1


def damping(depths, own_waves, first, span):
    degree = (own_waves[:, None] + first + jnp.arange(span, dtype=jnp.int32)[None, :]).astype(
        jnp.float32
    )
    return 1.0 / (
        1.0
        + depths[None, :, None] * degree[:, None, :] * (degree[:, None, :] + 1.0) / float(NT * NT)
    )


def inverse_legendre(spectral, legendre, own_lengths):
    wave_local, channels, lev_local, spec_len = spectral.shape
    half_lat = legendre.shape[1]
    row_total = channels * lev_local
    block_width = min(256, spec_len)

    def inverse_per_wave(column, result):
        coeffs = spectral[column].reshape(row_total, spec_len)
        polys = legendre[column]
        length = own_lengths[column]
        blocks = (length + block_width - 1) // block_width

        def inverse_per_block(block_no, sums_pair):
            offset = block_no * block_width
            segment = lax.dynamic_slice_in_dim(coeffs, offset, block_width, 1)
            poly_block = lax.dynamic_slice_in_dim(polys, offset, block_width, 1)
            position = offset + jnp.arange(block_width, dtype=jnp.int32)
            segment = jnp.where(position[None, :] < length, segment, jnp.zeros_like(segment))
            even_sum, odd_sum = sums_pair
            even_piece = jnp.where(position[None, :] % 2 == 0, segment, jnp.zeros_like(segment))
            odd_piece = jnp.where(position[None, :] % 2 == 1, segment, jnp.zeros_like(segment))
            contract = (((1,), (1,)), ((), ()))
            even_sum = even_sum + lax.dot_general(
                even_piece, poly_block, contract, preferred_element_type=jnp.float32
            )
            odd_sum = odd_sum + lax.dot_general(
                odd_piece, poly_block, contract, preferred_element_type=jnp.float32
            )
            return (even_sum, odd_sum)

        zeros_init = jnp.zeros((row_total, half_lat), jnp.float32)
        even_sum, odd_sum = lax.fori_loop(0, blocks, inverse_per_block, (zeros_init, zeros_init))
        northern = even_sum + odd_sum
        southern = jnp.flip(even_sum - odd_sum, axis=1)
        joined = jnp.concatenate([northern, southern], axis=1).astype(jnp.bfloat16)
        return result.at[column].set(joined.reshape(channels, lev_local, 2 * half_lat))

    start_value = jnp.zeros((wave_local, channels, lev_local, 2 * half_lat), jnp.bfloat16)
    return lax.fori_loop(0, wave_local, inverse_per_wave, start_value)


def forward_legendre(returned, legendre, own_lengths, cycle_weights):
    wave_local, channels, lev_local, lat_total = returned.shape
    half_lat = legendre.shape[1]
    spec_len = legendre.shape[2]
    row_total = channels * lev_local
    block_width = min(256, spec_len)
    northern = returned[..., :half_lat].astype(jnp.float32)
    southern = jnp.flip(returned[..., half_lat:], axis=3).astype(jnp.float32)
    even_part = (
        (cycle_weights * (northern + southern))
        .astype(jnp.bfloat16)
        .reshape(wave_local, row_total, half_lat)
    )
    odd_part = (
        (cycle_weights * (northern - southern))
        .astype(jnp.bfloat16)
        .reshape(wave_local, row_total, half_lat)
    )

    def forward_per_wave(column, result):
        polys = legendre[column]
        length = own_lengths[column]
        even_rows = even_part[column]
        odd_rows = odd_part[column]
        blocks = (length + block_width - 1) // block_width

        def forward_per_block(block_no, coeffs):
            offset = block_no * block_width
            poly_block = lax.dynamic_slice_in_dim(polys, offset, block_width, 1)
            position = offset + jnp.arange(block_width, dtype=jnp.int32)
            from_even = jnp.dot(even_rows, poly_block, preferred_element_type=jnp.float32)
            from_odd = jnp.dot(odd_rows, poly_block, preferred_element_type=jnp.float32)
            values = jnp.where(position[None, :] % 2 == 0, from_even, from_odd)
            values = jnp.where(position[None, :] < length, values, 0.0).astype(jnp.bfloat16)
            return lax.dynamic_update_slice_in_dim(coeffs, values, offset, 1)

        coeffs = lax.fori_loop(
            0, blocks, forward_per_block, jnp.zeros((row_total, spec_len), jnp.bfloat16)
        )
        return result.at[column].set(coeffs.reshape(channels, lev_local, spec_len))

    start_value = jnp.zeros((wave_local, channels, lev_local, spec_len), jnp.bfloat16)
    return lax.fori_loop(0, wave_local, forward_per_wave, start_value)


def on_device(
    spectral,
    legendre,
    wave_ids,
    trunc_lengths,
    cycle_points,
    grid_coef,
    cycle_weights,
    modes_in,
    modes_out,
    depths,
):
    wave_rank = lax.axis_index("wave")
    lev_rank = lax.axis_index("lev")
    wave_local, channels, lev_local, spec_len = spectral.shape
    own_waves = lax.dynamic_slice_in_dim(wave_ids, wave_rank * wave_local, wave_local)
    own_lengths = lax.dynamic_slice_in_dim(trunc_lengths, wave_rank * wave_local, wave_local)
    fourier = inverse_legendre(spectral, legendre, own_lengths)
    band_block = lax.all_to_all(fourier, "wave", split_axis=3, concat_axis=0, tiled=True)
    wave_total, chan_count, items, band = band_block.shape
    group_size = cycle_group_size()
    groups = band // group_size
    cycle_count = lax.dynamic_slice_in_dim(cycle_points, wave_rank * band, band)
    stacked = jnp.moveaxis(
        band_block.reshape(wave_total, chan_count, items, groups, group_size), 3, 0
    )
    counts = cycle_count.reshape(groups, group_size)
    coefs = grid_coef.reshape(groups, group_size, grid_coef.shape[1])

    def per_group(packed):
        return cycle_trip(packed[0], wave_ids, packed[1], packed[2])

    results = lax.map(per_group, (stacked, counts, coefs))
    analysed = jnp.moveaxis(results, 0, 3).reshape(wave_total, chan_count, items, band)
    returned = lax.all_to_all(analysed, "wave", split_axis=0, concat_axis=3, tiled=True)
    projected = forward_legendre(returned, legendre, own_lengths, cycle_weights)
    mode_vals = jnp.einsum(
        "kl,mcli->mcki",
        modes_in,
        lax.all_gather(projected, "lev", axis=2, tiled=True),
        preferred_element_type=jnp.float32,
    )
    damp = damping(depths, own_waves, 0, spec_len)
    scaled = (mode_vals * damp[:, None, :, :]).astype(jnp.bfloat16)
    own_rows = lax.dynamic_slice_in_dim(modes_out, lev_rank * lev_local, lev_local, 0)
    update = jnp.einsum(
        "lk,mcki->mcli", own_rows, scaled, preferred_element_type=jnp.float32
    ).astype(jnp.bfloat16)
    return update


def solution(mesh):
    placed = (
        P("wave", None, "lev", None),
        P("wave", None, None),
        P(),
        P(),
        P(),
        P("wave", None),
        P(),
        P(),
        P(),
        P(),
    )
    return jax.shard_map(
        on_device,
        mesh=mesh,
        in_specs=placed,
        out_specs=P("wave", None, "lev", None),
        check_vma=False,
    )
```

profile of v0, /device:TPU:0, one launch (start us, length us, event | category | flops | bytes accessed | tf_op | source)
XLA Modules:
  0.0 752.5 jit_solution(11752609533973577383)
XLA Ops:
  7.4 46.6 %while.138 = (s32[]{:T(128)}, bf16[4,6,16,1280]{3,2,1,0:T(8,128)(2,1)S(1)}, s32[4]{0:T(128)S(1)}, bf16[4,6,16,1280]{3,2,1,0:T(8,128)(2,1)}, bf16[4,640,1280]{2,1...) while((s32[]{:T(128)}, ...), condition=%wide.region_4.5_spmd, body=%wide.region_0.4_spmd.sunk | while | flops 63941424 | bytes 8213980 | solution.py:105
  11.2 6.0 while.142
  23.2 6.0 while.142
  35.1 6.0 while.142
  54.0 7.7 %copy.30 = bf16[4,6,16,1280]{2,0,1,3:T(4,128)(2,1)} copy(bf16[4,6,16,1280]{3,2,1,0:T(8,128)(2,1)S(1)} %get-tuple-element.681) | data formatting | bytes 1966080 | tf_op jit(solution)/shard_map/while | solution.py:105
  61.7 10.8 %reshape.620 = bf16[8,2,30720]{2,1,0:T(2,128)(2,1)} reshape(bf16[1280,6,4,16]{3,2,1,0:T(4,128)(2,1)} %bitcast.142) | data formatting | bytes 1966080
  77.1 24.2 %all-to-all-done = bf16[8,2,30720]{2,1,0:T(2,128)(2,1)S(1)} async-done(((bf16[8,2,30720]{2,1,0:T(2,128)(2,1)}), bf16[8,2,30720]{2,1,0:T(2,128)(2,1)S(1)}, u32[]{:S(2)}, u32[]{:S(2)}) %all-to-all-start) | async-done | bytes 983072 | tf_op jit(solution)/shard_map/all_to_all | solution.py:171
  101.2 7.2 reshape.621
  108.5 8.4 %copy.31 = bf16[4,6,16,8,160]{2,4,1,0,3:T(8,128)(2,1)} copy(bf16[4,6,16,8,160]{2,0,1,4,3:T(4,128)(2,1)} %bitcast.143) | data formatting | bytes 1966080 | tf_op jit(solution)/shard_map/all_to_all | solution.py:171
  116.8 9.7 %copy.32 = bf16[20,32,6,16,8]{1,4,3,2,0:T(8,128)(2,1)} copy(bf16[20,32,6,16,8]{3,4,0,2,1:T(8,128)(2,1)} %bitcast.144) | data formatting | bytes 1966080 | tf_op jit(solution)/shard_map/while | solution.py:185
  126.5 488.3 %while.139 = (s32[]{:T(128)}, bf16[20,32,6,16,8]{1,3,2,4,0:T(8,128)(2,1)}, s32[20,8]{1,0:T(8,128)S(1)}, s32[32]{0:T(128)S(1)}, bf16[20,32,6,16,8]{1,4,3,2,0:T(8,128)(2,1)}, /*index=5*/f32[20,8,2560]{2,1,0:T(8,128)}, s32[]{:T(128)}) while((s32[]{:T(128)}, bf16[20,32,6,16,8]{1,3,2,4,0:T(8,128)(2,1)}, s32[20,8]{1,0:T(8,128)S(1)}, ...), condition=%wide.region_6.7_spmd, body=%wide.region_5.6_spmd.sunk | while | flops 270372576 | bytes 39293648 | solution.py:185
  130.4 5.0 multiply_subtract_fusion.2
  154.8 5.0 multiply_subtract_fusion.2
  203.6 5.0 multiply_subtract_fusion.2
  228.1 5.0 multiply_subtract_fusion.2
  252.5 5.0 multiply_subtract_fusion.2
  276.9 5.0 multiply_subtract_fusion.2
  301.3 5.0 multiply_subtract_fusion.2
  325.7 5.0 multiply_subtract_fusion.2
  374.5 5.0 multiply_subtract_fusion.2
  398.9 5.0 multiply_subtract_fusion.2
  447.7 5.0 multiply_subtract_fusion.2
  472.2 5.0 multiply_subtract_fusion.2
  496.6 5.0 multiply_subtract_fusion.2
  521.0 5.0 multiply_subtract_fusion.2
  614.8 6.2 copy.34
  624.9 37.0 %all-to-all-done.1 = bf16[32,6,16,160]{3,2,1,0:T(8,128)(2,1)S(1)} async-done(((bf16[32,6,16,160]{3,2,1,0:T(8,128)(2,1)}), bf16[32,6,16,160]{3,2,1,0:T(8,128)(2,1)S(1)}, u32[]{:S(2)}, u32[]{:S(2)}) %all-to-all-start.1) | async-done | bytes 983072 | tf_op jit(solution)/shard_map/all_to_all | solution.py:187
  666.6 42.1 %while.141 = (s32[]{:T(128)}, bf16[4,6,16,1280]{3,2,1,0:T(8,128)(2,1)S(1)}, s32[4]{0:T(128)S(1)}, bf16[4,640,1280]{2,1,0:T(8,128)(2,1)}, bf16[4,96,640]{2,1,0:T(...) while((s32[]{:T(128)}, ...), condition=%wide.region_11.12_spmd, body=%wide.region_7.11_spmd.sunk | while | flops 63090224 | bytes 5803138 | solution.py:150
  670.5 5.5 while.143
  681.3 5.5 while.143
  692.1 5.5 while.143
  710.2 30.6 %all-gather.2.cloned.1.call-done = bf16[4,6,64,1280]{3,2,1,0:T(8,128)(2,1)} async-done(((bf16[4,6,16,1280]{3,2,1,0:T(8,128)(2,1)}), bf16[4,6,64,1280]{3,2,1,0:T(8,128)(2,1)}) %all-gather.2.cloned.1.call-update) | async-done | bytes 3932176 | tf_op jit(solution)/shard_map/all_gather | solution.py:192
  (705 shorter events, 527.5 us)
Async XLA Ops:
  6.5 734.3 %copy-start = (bf16[64,64]{1,0:T(8,128)(2,1)S(1)}, bf16[64,64]{1,0:T(8,128)(2,1)}, u32[]{:S(2)}) copy-start(bf16[64,64]{1,0:T(8,128)(2,1)} %param.31) | copy-start | bytes 24580
  11.2 6.6 copy-start.3
  23.2 6.6 copy-start.3
  35.1 6.6 copy-start.3
  47.1 5.4 copy-start.3
  72.5 28.8 %all-to-all-start = ((bf16[8,2,30720]{2,1,0:T(2,128)(2,1)}), bf16[8,2,30720]{2,1,0:T(2,128)(2,1)S(1)}, u32[]{:S(2)}, u32[]{:S(2)}) async-start(bf16[8,2,30720]{2,1,0:T(2,128)(2,1)} %reshape.620), calls=%async_computation | async-start | bytes 1966080 | tf_op jit(solution)/shard_map/all_to_all | solution.py:171
  116.8 9.7 %copy-start.2 = (s32[32]{0:T(128)S(1)}, s32[32]{0:T(128)}, u32[]{:S(2)}) copy-start(s32[32]{0:T(128)} %param.26) | copy-start | bytes 388
  621.0 40.9 %all-to-all-start.1 = ((bf16[32,6,16,160]{3,2,1,0:T(8,128)(2,1)}), bf16[32,6,16,160]{3,2,1,0:T(8,128)(2,1)S(1)}, u32[]{:S(2)}, u32[]{:S(2)}) async-start(bf16[32,6,16,160]{3,2,1,0:T(8,128)(2,1)} %copy.34), calls=%async_computation.1 | async-start | bytes 3145728 | tf_op jit(solution)/shard_map/all_to_all | solution.py:187
  624.6 116.2 %all-gather.2.cloned.1.call-start = ((), (), s32[]{:S(2)}) async-start(), calls=%async_computation.2 | async-start | bytes 4915200 | tf_op jit(solution)/shard_map/all_gather | solution.py:192
  662.8 2.5 copy-start.5
  664.5 2.1 copy-start.4
  666.6 43.3 %copy-start.6 = (f32[64]{0:T(128)S(1)}, f32[64]{0:T(128)}, u32[]{:S(2)}) copy-start(f32[64]{0:T(128)} %param.33) | copy-start | bytes 772
  708.7 0.9 copy-start.1
Sparse Core Ops, SparseCore 0:
  709.8 30.9 all-gather.1
where the time goes:
time: 756 us; the launch traced here: 752 us
  local copies, waits for them, and re-layouts  279 us (37%)
  other arithmetic  267 us (35%)
  waiting for transfers between devices  91.8 us (12%)
  matrix products  84.7 us (11%)
  between operations  13.5 us (2%)
  loops' own time  8.98 us (1%)
  starting transfers between devices  7.61 us (1%)
    sub x20, other arithmetic, trig_rows(): cos_high * cos_low - sin_high * sin_low  99.9 us
    neg x20, local copies, waits for them, and re-layouts, trig_rows(): sine_part = jnp.where(live_mask, -sine, 0.0)  88.2 us
    another operation x32, other arithmetic  55.4 us
    sub x20, local copies, waits for them, and re-layouts, trig_rows(): cos_high * cos_low - sin_high * sin_low  49.5 us
    dot_general x20, matrix products, cycle_trip(): jnp.einsum('gfik,grmk->mrfig', tendency, polys, preferred_element_type=jn...  48 us
    all_to_all x1, waiting for transfers between devices, on_device(): lax.all_to_all(analysed, 'wave', split_axis=0, concat_axis=3, tiled=True)  37 us
    cos x20, other arithmetic, trig_rows(): cos_low = jnp.cos(low_angle)[:, :, None, :]  36.6 us
    cos x20, other arithmetic, trig_rows(): cos_high = jnp.cos(high_angle)[:, :, :, None]  36.5 us
  transfers between devices with their start and end apart: 3, of which 3 were waited for; matrix products, arithmetic and copies ran while one was open for 0% of the time, Pallas kernels for 0%

commit v1 on v0

v1 whole, which is shorter than its diff:
```python
import functools

import jax
import jax.numpy as jnp
import numpy as np
from jax import lax
from jax.experimental import pallas as pl
from jax.experimental.pallas import tpu as pltpu
from jax.sharding import PartitionSpec as P

NT = 1280
LOW = 256
LANES = 128
NN = (((1,), (0,)), ((), ()))
NTD = (((1,), (1,)), ((), ()))
TN = (((0,), (0,)), ((), ()))
F32 = jnp.float32
BF16 = jnp.bfloat16


def turn_coefs(func, degree):
    nodes = 0.125 * (1.0 + np.cos(np.pi * (np.arange(degree + 1) + 0.5) / (degree + 1)))
    cheb = np.polynomial.Chebyshev.fit(nodes, func(nodes), degree, domain=[0.0, 0.25])
    return [float(v) for v in cheb.convert(kind=np.polynomial.Polynomial).coef]


COS = turn_coefs(lambda u: np.cos(2 * np.pi * np.sqrt(u)), 6)
SIN = turn_coefs(lambda u: np.sin(2 * np.pi * np.sqrt(u)) / np.sqrt(u), 6)


def horner(coefs, u):
    total = jnp.full_like(u, coefs[-1])
    for value in coefs[-2::-1]:
        total = total * u + value
    return total


def cos_sin(product, points, inverse):
    rest = product - jnp.round(product * inverse) * points
    turn = rest * inverse
    square = turn * turn
    return horner(COS, square), horner(SIN, square) * turn


def pad_to(value, unit):
    return -(-value // unit) * unit


def inverse_kernel(lengths, spec_ref, leg_ref, out_ref):
    shards, _, band, rows = out_ref.shape
    half = shards // 2
    length = lengths[pl.program_id(0)]
    _, channels, items, span = spec_ref.shape
    coeffs = spec_ref[0].reshape(rows, span)
    place = lax.broadcasted_iota(jnp.int32, (rows, span), 1)
    live = jnp.where(place < length, coeffs.astype(F32), 0.0)
    sign = jnp.where(place % 2 == 0, live, -live).astype(BF16)
    live = live.astype(BF16)
    wide = pad_to(rows, LANES)
    parts = [live, sign]
    if wide > rows:
        fill = jnp.zeros((wide - rows, span), BF16)
        parts = [live, fill, sign, fill]
    both = jnp.concatenate(parts, axis=0)
    for part in range(half):
        polys = leg_ref[0, part * band : (part + 1) * band, :]
        sums = lax.dot_general(polys, both, NTD, preferred_element_type=F32)
        out_ref[part, 0] = sums[:, :rows].astype(BF16)
        out_ref[shards - 1 - part, 0] = sums[:, wide : wide + rows].astype(BF16)


def inverse_legendre(spectral, legendre, lengths, shards):
    waves, channels, items, span = spectral.shape
    half_lat = legendre.shape[1]
    band = 2 * half_lat // shards
    rows = channels * items
    return pl.pallas_call(
        inverse_kernel,
        name="inverse",
        out_shape=jax.ShapeDtypeStruct((shards, waves, band, rows), BF16),
        grid_spec=pltpu.PrefetchScalarGridSpec(
            num_scalar_prefetch=1,
            grid=(waves,),
            in_specs=[
                pl.BlockSpec((1, channels, items, span), lambda m, s: (m, 0, 0, 0)),
                pl.BlockSpec((1, half_lat, span), lambda m, s: (m, 0, 0)),
            ],
            out_specs=pl.BlockSpec((shards, 1, band, rows), lambda m, s: (0, m, 0, 0)),
        ),
        compiler_params=pltpu.CompilerParams(vmem_limit_bytes=40 << 20),
        cost_estimate=pl.CostEstimate(
            flops=4 * waves * rows * half_lat * span,
            bytes_accessed=2 * waves * half_lat * span,
            transcendentals=0,
        ),
    )(lengths, spectral, legendre)


def forward_kernel(lengths, values_ref, leg_ref, weight_ref, out_ref):
    shards, _, band, rows = values_ref.shape
    half = shards // 2
    span = leg_ref.shape[2]
    length = lengths[pl.program_id(0)]
    north = jnp.concatenate([values_ref[k, 0] for k in range(half)], axis=0).astype(F32)
    south = jnp.concatenate(
        [values_ref[shards - 1 - k, 0] for k in range(half)], axis=0
    ).astype(F32)
    weights = weight_ref[:, :1]
    even = (weights * (north + south)).astype(BF16)
    odd = (weights * (north - south)).astype(BF16)
    polys = leg_ref[0]
    from_even = lax.dot_general(even, polys, TN, preferred_element_type=F32)
    from_odd = lax.dot_general(odd, polys, TN, preferred_element_type=F32)
    place = lax.broadcasted_iota(jnp.int32, (rows, span), 1)
    values = jnp.where(place % 2 == 0, from_even, from_odd)
    out_ref[0] = jnp.where(place < length, values, 0.0).astype(BF16)


def forward_legendre(returned, legendre, lengths, weights):
    shards, waves, band, rows = returned.shape
    half_lat, span = legendre.shape[1:]
    spread = jnp.broadcast_to(weights[:, None], (half_lat, LANES))
    return pl.pallas_call(
        forward_kernel,
        name="forward",
        out_shape=jax.ShapeDtypeStruct((waves, rows, span), BF16),
        grid_spec=pltpu.PrefetchScalarGridSpec(
            num_scalar_prefetch=1,
            grid=(waves,),
            in_specs=[
                pl.BlockSpec((shards, 1, band, rows), lambda m, s: (0, m, 0, 0)),
                pl.BlockSpec((1, half_lat, span), lambda m, s: (m, 0, 0)),
                pl.BlockSpec((half_lat, LANES), lambda m, s: (0, 0)),
            ],
            out_specs=pl.BlockSpec((1, rows, span), lambda m, s: (m, 0, 0)),
        ),
        compiler_params=pltpu.CompilerParams(vmem_limit_bytes=40 << 20),
        cost_estimate=pl.CostEstimate(
            flops=4 * waves * rows * half_lat * span,
            bytes_accessed=2 * waves * half_lat * span,
            transcendentals=0,
        ),
    )(lengths, returned, legendre, spread)


def cycle_kernel(
    fields, flip, points, inverses, in_ref, coef_ref, lane_ref, wave_ref, pick_ref, merge_ref, out_ref
):
    block, waves, both_rows = in_ref.shape
    rows = both_rows // 2
    items = rows // fields
    lon_max = coef_ref.shape[1]
    chunks = lon_max // LOW
    steps = pad_to(chunks, 8)
    wide = 4 * waves
    first = pl.program_id(0) * block
    reverse = flip[0]
    wave_lane = lane_ref[0:1, :]
    step_no = lax.broadcasted_iota(jnp.int32, (steps, wide), 0).astype(F32)
    step_wave = step_no * (wave_lane * float(LOW))
    low_no = lax.broadcasted_iota(jnp.int32, (waves, LOW), 1)
    low_wave = low_no.astype(F32) * wave_ref[...]
    wave_col = wave_ref[...]
    row_lane = lax.broadcasted_iota(jnp.int32, (waves, both_rows), 1)
    out_lane = lax.broadcasted_iota(jnp.int32, (rows, 2 * waves), 1)
    place = lax.broadcasted_iota(jnp.int32, (rows, LOW), 1).astype(F32)

    def one(local, carry):
        pts = points[first + local]
        inv = inverses[first + local]
        seat = local + reverse * (block - 1 - 2 * local)
        cos_step, sin_step = cos_sin(step_wave, pts, inv)
        synth = cos_step * lane_ref[1:2, :] + sin_step * lane_ref[2:3, :]
        anal = cos_step * lane_ref[3:4, :] + sin_step * lane_ref[4:5, :]
        cos_low, sin_low = cos_sin(low_wave, pts, inv)
        shown = 2.0 * wave_col < pts
        cos_low = jnp.where(shown, cos_low, 0.0).astype(BF16)
        sin_low = jnp.where(shown, -sin_low, 0.0).astype(BF16)
        table_in = jnp.concatenate([cos_low, sin_low, cos_low, sin_low], axis=0)
        table_out = jnp.concatenate([cos_low, sin_low, sin_low, cos_low], axis=0)

        data = in_ref[seat].astype(F32)
        real = jnp.where(row_lane < rows, data, 0.0).astype(BF16)
        imag = jnp.where(row_lane < rows, 0.0, data).astype(BF16)
        four = jnp.concatenate([real, imag, imag, real], axis=0)
        spread = lax.dot_general(pick_ref[...], four, NTD, preferred_element_type=F32)
        turned = jnp.concatenate(
            [(spread * synth[k : k + 1, :]).astype(BF16) for k in range(chunks)], axis=0
        )
        grid = lax.dot_general(turned, table_in, NN, preferred_element_type=F32)
        pieces = []
        for k in range(chunks):
            vals = grid[k * rows : (k + 1) * rows]
            after = jnp.concatenate([vals[items:], vals[:items]], axis=0)
            coef = coef_ref[pl.ds(local, 1), k * LOW : (k + 1) * LOW]
            tend = vals * (coef + after)
            pieces.append(jnp.where(place < pts - float(k * LOW), tend, 0.0).astype(BF16))
        tend = jnp.concatenate(pieces, axis=0)
        back = lax.dot_general(tend, table_out, NTD, preferred_element_type=F32)
        total = back[:rows] * anal[0:1, :]
        for k in range(1, chunks):
            total = total + back[k * rows : (k + 1) * rows] * anal[k : k + 1, :]
        result = (total[:, : 2 * waves] + total[:, 2 * waves :]) * inv
        split = jnp.concatenate(
            [
                jnp.where(out_lane < waves, result, 0.0).astype(BF16),
                jnp.where(out_lane < waves, 0.0, result).astype(BF16),
            ],
            axis=0,
        )
        out_ref[seat] = lax.dot_general(
            merge_ref[...], split, NTD, preferred_element_type=F32
        ).astype(BF16)
        return carry

    lax.fori_loop(0, block, one, 0, unroll=2)


def cycle_trips(values, wave_ids, points, coef, flip, fields):
    band, waves, both_rows = values.shape
    rows = both_rows // 2
    wide = 4 * waves
    lon_max = coef.shape[1]
    block = next(c for c in (40, 32, 16, 8) if band % c == 0)
    blocks = band // block
    lane = jnp.arange(wide)
    part = lane // waves
    wave_lane = jnp.tile(wave_ids, 4).astype(F32)
    factor = jnp.where(wave_lane == 0, 1.0, 2.0)
    own = (part < 2).astype(F32)
    cross = jnp.where(part == 2, -1.0, jnp.where(part == 3, 1.0, 0.0))
    zero = jnp.zeros_like(own)
    lanes = jnp.stack(
        [wave_lane, own * factor, cross * factor, own, -cross, zero, zero, zero], axis=0
    )
    wave_col = jnp.broadcast_to(wave_ids.astype(F32)[:, None], (waves, LOW))
    pick = (jnp.arange(rows)[:, None] == jnp.arange(both_rows)[None, :] % rows).astype(BF16)
    merge = (jnp.arange(waves)[:, None] == jnp.arange(2 * waves)[None, :] % waves).astype(BF16)

    def seat(b, s, *_):
        return (b + s[0] * (blocks - 1 - 2 * b), 0, 0)

    whole = lambda b, *_: (0, 0)
    return pl.pallas_call(
        functools.partial(cycle_kernel, fields),
        name="cycles",
        out_shape=jax.ShapeDtypeStruct((band, waves, both_rows), BF16),
        grid_spec=pltpu.PrefetchScalarGridSpec(
            num_scalar_prefetch=3,
            grid=(blocks,),
            in_specs=[
                pl.BlockSpec((block, waves, both_rows), seat),
                pl.BlockSpec((block, lon_max), lambda b, *_: (b, 0)),
                pl.BlockSpec((8, wide), whole),
                pl.BlockSpec((waves, LOW), whole),
                pl.BlockSpec((rows, both_rows), whole),
                pl.BlockSpec((waves, 2 * waves), whole),
            ],
            out_specs=pl.BlockSpec((block, waves, both_rows), seat),
        ),
        compiler_params=pltpu.CompilerParams(vmem_limit_bytes=40 << 20),
        cost_estimate=pl.CostEstimate(
            flops=8 * band * waves * rows * lon_max,
            bytes_accessed=4 * band * lon_max,
            transcendentals=0,
        ),
    )(
        flip,
        points.astype(F32),
        1.0 / points.astype(F32),
        values,
        coef,
        lanes,
        wave_col,
        pick,
        merge,
    )


def mode_kernel(channels, waves, all_ref, in_ref, out_ref_modes, depth_ref, ids, update_ref):
    shards, _, rows, span = all_ref.shape
    items = rows // channels
    wave = ids[pl.program_id(0)]
    modes = in_ref.shape[0]
    place = lax.broadcasted_iota(jnp.int32, (modes, span), 1)
    degree = (place + wave).astype(F32)
    damp = 1.0 / (1.0 + depth_ref[:, :1] * degree * (degree + 1.0) / float(NT * NT))
    for c in range(channels):
        stack = jnp.concatenate(
            [all_ref[s, 0, c * items : (c + 1) * items, :] for s in range(shards)], axis=0
        )
        vals = lax.dot_general(in_ref[...], stack, NN, preferred_element_type=F32)
        scaled = (vals * damp).astype(BF16)
        update_ref[0, c] = lax.dot_general(
            out_ref_modes[...], scaled, NN, preferred_element_type=F32
        ).astype(BF16)


def vertical(gathered, modes_in, own_rows, depths, own_waves, channels):
    shards, waves, rows, span = gathered.shape
    items = rows // channels
    modes, levels = modes_in.shape
    spread = jnp.broadcast_to(depths[:, None], (modes, LANES))

    def body(ids, all_ref, in_ref, own_ref, depth_ref, update_ref):
        mode_kernel(channels, waves, all_ref, in_ref, own_ref, depth_ref, ids, update_ref)

    return pl.pallas_call(
        body,
        name="vertical",
        out_shape=jax.ShapeDtypeStruct((waves, channels, items, span), BF16),
        grid_spec=pltpu.PrefetchScalarGridSpec(
            num_scalar_prefetch=1,
            grid=(waves,),
            in_specs=[
                pl.BlockSpec((shards, 1, rows, span), lambda m, s: (0, m, 0, 0)),
                pl.BlockSpec((modes, levels), lambda m, s: (0, 0)),
                pl.BlockSpec((items, modes), lambda m, s: (0, 0)),
                pl.BlockSpec((modes, LANES), lambda m, s: (0, 0)),
            ],
            out_specs=pl.BlockSpec((1, channels, items, span), lambda m, s: (m, 0, 0, 0)),
        ),
        compiler_params=pltpu.CompilerParams(vmem_limit_bytes=40 << 20),
    )(own_waves, gathered, modes_in, own_rows, spread)


def on_device(
    spectral,
    legendre,
    wave_ids,
    trunc_lengths,
    cycle_points,
    grid_coef,
    cycle_weights,
    modes_in,
    modes_out,
    depths,
):
    wave_rank = lax.axis_index("wave")
    lev_rank = lax.axis_index("lev")
    shards = lax.axis_size("wave")
    waves, channels, items, span = spectral.shape
    rows = channels * items
    band = grid_coef.shape[0]
    own_waves = lax.dynamic_slice_in_dim(wave_ids, wave_rank * waves, waves)
    own_lengths = lax.dynamic_slice_in_dim(trunc_lengths, wave_rank * waves, waves)
    fourier = inverse_legendre(spectral, legendre, own_lengths, shards)
    arrived = lax.all_to_all(fourier, "wave", split_axis=0, concat_axis=0, tiled=True)
    by_cycle = jnp.swapaxes(arrived.reshape(shards * waves, band, rows), 0, 1)
    points = lax.dynamic_slice_in_dim(cycle_points, wave_rank * band, band)
    flip = (wave_rank >= shards // 2).astype(jnp.int32).reshape(1)
    analysed = cycle_trips(by_cycle, wave_ids, points, grid_coef, flip, channels // 2)
    leaving = jnp.swapaxes(analysed, 0, 1).reshape(shards, waves, band, rows)
    returned = lax.all_to_all(leaving, "wave", split_axis=0, concat_axis=0, tiled=True)
    projected = forward_legendre(returned, legendre, own_lengths, cycle_weights)
    gathered = lax.all_gather(projected, "lev", axis=0)
    own_rows = lax.dynamic_slice_in_dim(modes_out, lev_rank * items, items, 0)
    return vertical(gathered, modes_in, own_rows, depths, own_waves, channels)


def solution(mesh):
    placed = (
        P("wave", None, "lev", None),
        P("wave", None, None),
        P(),
        P(),
        P(),
        P("wave", None),
        P(),
        P(),
        P(),
        P(),
    )
    return jax.shard_map(
        on_device,
        mesh=mesh,
        in_specs=placed,
        out_specs=P("wave", None, "lev", None),
        check_vma=False,
    )
```

time: 756 us -> 251 us (0.33)
  local copies, waits for them, and re-layouts: 279 us -> 8.64 us
  other arithmetic: 267 us -> 0.84 us
  Pallas kernels: 0 us -> 123 us
  matrix products: 84.7 us -> 0 us
  blocking collectives: 0 us -> 35 us
  waiting for transfers between devices: 91.8 us -> 62.4 us
  loops' own time: 8.98 us -> 0 us
    pallas_call x0 -> x4, Pallas kernels: none -> 123 us  [the longest x1 107 us: cycle_trips(): pl.pallas_call(functools.partial(cycle_kernel, fields), name='cycles', ou...]
    sub x24 -> x0, other arithmetic: 100 us -> none  [the longest x20 99.9 us: trig_rows(): cos_high * cos_low - sin_high * sin_low]
    neg x20 -> x0, local copies, waits for them, and re-layouts: 88.2 us -> none  [trig_rows(): sine_part = jnp.where(live_mask, -sine, 0.0)]
    dot_general x117 -> x0, matrix products: 84.7 us -> none  [the longest x20 48 us: cycle_trip(): jnp.einsum('gfik,grmk->mrfig', tendency, polys, preferred_element_type=jn...]
    cos x40 -> x0, other arithmetic: 73.1 us -> none  [the longest x20 36.6 us: trig_rows(): cos_low = jnp.cos(low_angle)[:, :, None, :]]
    another operation x32 -> x0, other arithmetic: 55.4 us -> none
    sub x20 -> x0, local copies, waits for them, and re-layouts: 49.5 us -> none  [trig_rows(): cos_high * cos_low - sin_high * sin_low]
    all_to_all x0 -> x1, blocking collectives: none -> 35 us  [on_device(): lax.all_to_all(leaving, 'wave', split_axis=0, concat_axis=0, tiled=True)]
  transfers between devices with their start and end apart: 3 -> 2, of which waited for: 3 -> 2; matrix products, arithmetic and copies ran while one was open for 0% -> 0% of each run, Pallas kernels for 0% -> 0%
where the time goes in v1:
time: 251 us
  Pallas kernels  123 us (49%)
  waiting for transfers between devices  62.4 us (25%)
  blocking collectives  35 us (14%)
  between operations  13.6 us (5%)
  local copies, waits for them, and re-layouts  8.64 us (3%)
  starting transfers between devices  7.48 us (3%)
    pallas_call x1, Pallas kernels, cycle_trips(): pl.pallas_call(functools.partial(cycle_kernel, fields), name='cycles', ou...  107 us
    all_to_all x1, blocking collectives, on_device(): lax.all_to_all(leaving, 'wave', split_axis=0, concat_axis=0, tiled=True)  35 us
    all_gather x1, waiting for transfers between devices, on_device(): gathered = lax.all_gather(projected, 'lev', axis=0)  32.1 us
    all_to_all x1, waiting for transfers between devices, on_device(): lax.all_to_all(fourier, 'wave', split_axis=0, concat_axis=0, tiled=True)  30.3 us
    all_to_all x1, starting transfers between devices, on_device(): lax.all_to_all(fourier, 'wave', split_axis=0, concat_axis=0, tiled=True)  7.44 us
    unnamed x22, local copies, waits for them, and re-layouts  6.22 us
    pallas_call x1, Pallas kernels, vertical(): pl.pallas_call(body, name='vertical', out_shape=jax.ShapeDtypeStruct((wav...  6.21 us
  transfers between devices with their start and end apart: 2, of which 2 were waited for; matrix products, arithmetic and copies ran while one was open for 0% of the time, Pallas kernels for 0%

profile of v1, /device:TPU:0, one launch (start us, length us, event | category | flops | bytes accessed | tf_op | source)
XLA Modules:
  0.0 250.8 jit_solution(5842988984332617759)
XLA Ops:
  6.5 0.0 copy-start
  6.5 0.7 dynamic_slice.13.lengths
  7.3 2.9 %copy-done.1 = bf16[4,640,1280]{2,1,0:T(8,128)(2,1)S(1)} copy-done((bf16[4,640,1280]{2,1,0:T(8,128)(2,1)S(1)}, bf16[4,640,1280]{2,1,0:T(8,128)(2,1)}, u32[]{:S(2)}) %copy-start.1) | copy-done | bytes 6553624
  10.1 1.2 copy-done.3
  11.3 5.0 %inverse.1 = bf16[8,4,160,96]{3,2,1,0:T(8,128)(2,1)} custom-call(s32[4]{0:T(128)S(1)} %dynamic_slice.13.lengths, bf16[4,6,16,1280]{3,2,1,0:T(8,128)(2,1)S(1)} %copy-done.3, bf16[4,640,1280]{2,1,0:T(8,128)(2,1)S(1)} %copy-done.1), custom_call_target="tpu_custom_call" | custom-call | flops 1258291200 | bytes 6553600 | tf_op jit(solution)/shard_map/inverse/pallas_call | solution.py:77
  16.3 7.4 %all-to-all-start = ((bf16[8,4,160,96]{3,2,1,0:T(8,128)(2,1)}), bf16[8,4,160,96]{3,2,1,0:T(8,128)(2,1)S(1)}, u32[]{:S(2)}, u32[]{:S(2)}) async-start(bf16[8,4,160,96]{3,2,1,0:T(8,128)(2,1)} %inverse.1), calls=%async_computation | async-start | bytes 2621440 | tf_op jit(solution)/shard_map/all_to_all | solution.py:348
  23.8 0.0 all-gather.3.cloned.1.call-start
  23.8 0.0 copy-done.8
  23.9 0.1 convert_element_type.46
  24.1 0.8 broadcast_divide_fusion
  24.9 0.0 copy-start.5
  24.9 30.3 %all-to-all-done = bf16[8,4,160,96]{3,2,1,0:T(8,128)(2,1)S(1)} async-done(((bf16[8,4,160,96]{3,2,1,0:T(8,128)(2,1)}), bf16[8,4,160,96]{3,2,1,0:T(8,128)(2,1)S(1)}, u32[]{:S(2)}, u32[]{:S(2)}) %all-to-all-start) | async-done | bytes 983072 | tf_op jit(solution)/shard_map/all_to_all | solution.py:348
  55.2 0.7 copy.13
  55.8 0.1 broadcast_in_dim.39.wave_ref
  55.9 0.0 copy-done.5
  55.9 106.8 %cycles.1 = bf16[160,32,96]{2,1,0:T(8,128)(2,1)S(1)} custom-call(s32[1]{0:T(128)} %bitcast.flip, f32[160]{0:T(256)S(1)} %get-tuple-element.6.points, f32[160]{0:T(256)S(1)} %get-tuple-element.5.inverses, bf16[160,32,96]{2,1,0:T(8,128)(2,1)S(1)} %bitcast.10, f32[160,2560]{1,0:T(8,128)S(1)} %copy-done.5, f32[8,128]{1,0:T(8,128)S(1)} %stack.5.lane_ref, ...), custom_call_target="tpu_custom_call" | custom-call | flops 5033164800 | bytes 1638400 | tf_op jit(solution)/shard_map/cycles/pallas_call | solution.py:244
  162.7 0.5 copy.14
  163.3 0.0 copy-start.6
  163.3 35.0 %all_to_all.10.values_ref = bf16[8,4,160,96]{3,2,1,0:T(8,128)(2,1)S(1)} all-to-all(bf16[8,4,160,96]{3,2,1,0:T(8,128)(2,1)S(1)} %bitcast.12), channel_id=1, replica_groups=mesh['wave'=8,'lev'=4] {'wave'}, dimensions={0} | all-to-all | bytes 1966080 | tf_op jit(solution)/shard_map/all_to_all | solution.py:354
  198.2 0.0 copy-done.6
  198.2 0.1 broadcast_in_dim.40.weight_ref
  198.4 0.0 slice-done
  198.4 0.0 copy-start.7
  198.4 0.0 copy-start.4
  198.4 4.9 %forward.1 = bf16[4,96,1280]{2,1,0:T(8,128)(2,1)} custom-call(s32[4]{0:T(128)S(1)} %dynamic_slice.13.lengths, bf16[8,4,160,96]{3,2,1,0:T(8,128)(2,1)S(1)} %all_to_all.10.values_ref, bf16[4,640,1280]{2,1,0:T(8,128)(2,1)S(1)} %bitcast.8, f32[640,128]{1,0:T(8,128)S(1)} %broadcast_in_dim.40.weight_ref), custom_call_target="tpu_custom_call" | custom-call | flops 1258291200 | bytes 6553600 | tf_op jit(solution)/shard_map/forward/pallas_call | solution.py:123
  203.3 0.0 all-gather.3.cloned.1.call-update
  203.3 0.1 dynamic_slice.12.ids
  203.4 0.0 copy-done
  203.4 32.1 %all-gather.3.cloned.1.call-done = bf16[16,96,1280]{2,1,0:T(8,128)(2,1)} async-done(((bf16[4,96,1280]{2,1,0:T(8,128)(2,1)}), bf16[16,96,1280]{2,1,0:T(8,128)(2,1)}) %all-gather.3.cloned.1.call-update) | async-done | bytes 3932176 | tf_op jit(solution)/shard_map/all_gather | solution.py:356
  235.5 0.1 broadcast_in_dim.41.depth_ref
  235.6 2.1 copy-done.2
  237.7 6.2 %vertical.1 = bf16[4,6,16,1280]{3,2,1,0:T(8,128)(2,1)} custom-call(s32[4]{0:T(128)S(1)} %dynamic_slice.12.ids, bf16[4,4,96,1280]{3,2,1,0:T(8,128)(2,1)S(1)} %bitcast.9, bf16[64,64]{1,0:T(8,128)(2,1)S(1)} %copy-done.4, bf16[16,64]{1,0:T(8,128)(2,1)S(1)} %constant_dynamic-slice_fusion.own_ref, f32[64,128]{1,0:T(8,128)S(1)} %broadcast_in_dim.41.depth_ref), custom_call_target="tpu_custom_call" | custom-call | tf_op jit(solution)/shard_map/vertical/pallas_call | solution.py:308
  (23 shorter events, 0.1 us)
Async XLA Ops:
  6.5 196.9 %copy-start = (bf16[64,64]{1,0:T(8,128)(2,1)S(1)}, bf16[64,64]{1,0:T(8,128)(2,1)}, u32[]{:S(2)}) copy-start(bf16[64,64]{1,0:T(8,128)(2,1)} %param.18) | copy-start | bytes 24580
  7.3 2.9 %copy-start.1 = (bf16[4,640,1280]{2,1,0:T(8,128)(2,1)S(1)}, bf16[4,640,1280]{2,1,0:T(8,128)(2,1)}, u32[]{:S(2)}) copy-start(bf16[4,640,1280]{2,1,0:T(8,128)(2,1)} %leg_ref.3) | copy-start | bytes 19660804
  10.1 1.2 copy-start.3
  16.3 7.5 %copy-start.8 = (s32[32]{0:T(128)S(1)}, s32[32]{0:T(128)}, u32[]{:S(2)}) copy-start(s32[32]{0:T(128)} %param.12) | copy-start | bytes 388
  16.3 38.8 %all-to-all-start = ((bf16[8,4,160,96]{3,2,1,0:T(8,128)(2,1)}), bf16[8,4,160,96]{3,2,1,0:T(8,128)(2,1)S(1)}, u32[]{:S(2)}, u32[]{:S(2)}) async-start(bf16[8,4,160,96]{3,2,1,0:T(8,128)(2,1)} %inverse.1), calls=%async_computation | async-start | bytes 2621440 | tf_op jit(solution)/shard_map/all_to_all | solution.py:348
  23.8 211.7 %all-gather.3.cloned.1.call-start = ((), (), s32[]{:S(2)}) async-start(), calls=%async_computation.2 | async-start | bytes 4915200 | tf_op jit(solution)/shard_map/all_gather | solution.py:356
  24.9 31.1 %copy-start.5 = (f32[160,2560]{1,0:T(8,128)S(1)}, f32[160,2560]{1,0:T(8,128)}, u32[]{:S(2)}) copy-start(f32[160,2560]{1,0:T(8,128)} %coef_ref.1) | copy-start | bytes 4915204
  55.2 143.2 %slice-start = ((s8[6553600]{0:T(1024)(128)(4,1)}), s8[4194304]{0:T(1024)(128)(4,1)S(1)}, s32[]{:S(2)}) async-start(s8[6553600]{0:T(1024)(128)(4,1)} %bitcast.7), calls=%async_computation.3 | async-start | bytes 8388608
  55.9 142.5 %slice-start.1 = ((s8[6553600]{0:T(1024)(128)(4,1)}), s8[2359296]{0:T(1024)(128)(4,1)S(1)}, s32[]{:S(2)}) async-start(s8[6553600]{0:T(1024)(128)(4,1)} %bitcast.7), calls=%async_computation.4 | async-start | bytes 4718592
  163.3 35.0 %copy-start.6 = (f32[640]{0:T(1024)S(1)}, f32[640]{0:T(1024)}, u32[]{:S(2)}) copy-start(f32[640]{0:T(1024)} %param.16) | copy-start | bytes 7684
  198.4 37.1 %copy-start.7 = (f32[64]{0:T(128)S(1)}, f32[64]{0:T(128)}, u32[]{:S(2)}) copy-start(f32[64]{0:T(128)} %param.19) | copy-start | bytes 772
  198.4 37.2 %copy-start.4 = (bf16[64,64]{1,0:T(8,128)(2,1)S(1)}, bf16[64,64]{1,0:T(8,128)(2,1)}, u32[]{:S(2)}) copy-start(bf16[64,64]{1,0:T(8,128)(2,1)} %in_ref.1) | copy-start | bytes 24580
  235.6 2.1 copy-start.2
Sparse Core Ops, SparseCore 0:
  203.4 32.0 all-gather.2

commit v2 on v1

--- a/solution.py
+++ b/solution.py
@@ -11,6 +11,7 @@
 NT = 1280
 LOW = 256
 LANES = 128
+GROUP = 4
 NN = (((1,), (0,)), ((), ()))
 NTD = (((1,), (1,)), ((), ()))
 TN = (((0,), (0,)), ((), ()))
@@ -165,10 +166,9 @@
     out_lane = lax.broadcasted_iota(jnp.int32, (rows, 2 * waves), 1)
     place = lax.broadcasted_iota(jnp.int32, (rows, LOW), 1).astype(F32)
 
-    def one(local, carry):
+    def prepare(local):
         pts = points[first + local]
         inv = inverses[first + local]
-        seat = local + reverse * (block - 1 - 2 * local)
         cos_step, sin_step = cos_sin(step_wave, pts, inv)
         synth = cos_step * lane_ref[1:2, :] + sin_step * lane_ref[2:3, :]
         anal = cos_step * lane_ref[3:4, :] + sin_step * lane_ref[4:5, :]
@@ -176,18 +176,16 @@
         shown = 2.0 * wave_col < pts
         cos_low = jnp.where(shown, cos_low, 0.0).astype(BF16)
         sin_low = jnp.where(shown, -sin_low, 0.0).astype(BF16)
-        table_in = jnp.concatenate([cos_low, sin_low, cos_low, sin_low], axis=0)
-        table_out = jnp.concatenate([cos_low, sin_low, sin_low, cos_low], axis=0)
-
+        return pts, inv, synth, anal, cos_low, sin_low
+
+    def pick(seat):
         data = in_ref[seat].astype(F32)
         real = jnp.where(row_lane < rows, data, 0.0).astype(BF16)
         imag = jnp.where(row_lane < rows, 0.0, data).astype(BF16)
         four = jnp.concatenate([real, imag, imag, real], axis=0)
-        spread = lax.dot_general(pick_ref[...], four, NTD, preferred_element_type=F32)
-        turned = jnp.concatenate(
-            [(spread * synth[k : k + 1, :]).astype(BF16) for k in range(chunks)], axis=0
-        )
-        grid = lax.dot_general(turned, table_in, NN, preferred_element_type=F32)
+        return lax.dot_general(pick_ref[...], four, NTD, preferred_element_type=F32)
+
+    def tendency(grid, local, pts):
         pieces = []
         for k in range(chunks):
             vals = grid[k * rows : (k + 1) * rows]
@@ -195,25 +193,61 @@
             coef = coef_ref[pl.ds(local, 1), k * LOW : (k + 1) * LOW]
             tend = vals * (coef + after)
             pieces.append(jnp.where(place < pts - float(k * LOW), tend, 0.0).astype(BF16))
-        tend = jnp.concatenate(pieces, axis=0)
-        back = lax.dot_general(tend, table_out, NTD, preferred_element_type=F32)
+        return jnp.concatenate(pieces, axis=0)
+
+    def reduce(back, anal, inv):
         total = back[:rows] * anal[0:1, :]
         for k in range(1, chunks):
             total = total + back[k * rows : (k + 1) * rows] * anal[k : k + 1, :]
         result = (total[:, : 2 * waves] + total[:, 2 * waves :]) * inv
-        split = jnp.concatenate(
+        return jnp.concatenate(
             [
                 jnp.where(out_lane < waves, result, 0.0).astype(BF16),
                 jnp.where(out_lane < waves, 0.0, result).astype(BF16),
             ],
             axis=0,
         )
-        out_ref[seat] = lax.dot_general(
-            merge_ref[...], split, NTD, preferred_element_type=F32
-        ).astype(BF16)
+
+    def several(step, carry):
+        locals_ = [step * GROUP + g for g in range(GROUP)]
+        seats = [v + reverse * (block - 1 - 2 * v) for v in locals_]
+        made = [prepare(v) for v in locals_]
+        spreads = [pick(v) for v in seats]
+        turned = [
+            jnp.concatenate(
+                [(x * w[2][k : k + 1, :]).astype(BF16) for k in range(chunks)], axis=0
+            )
+            for x, w in zip(spreads, made)
+        ]
+        grids = [
+            lax.dot_general(
+                x,
+                jnp.concatenate([w[4], w[5], w[4], w[5]], axis=0),
+                NN,
+                preferred_element_type=F32,
+            )
+            for x, w in zip(turned, made)
+        ]
+        tends = [tendency(x, v, w[0]) for x, v, w in zip(grids, locals_, made)]
+        backs = [
+            lax.dot_general(
+                x,
+                jnp.concatenate([w[4], w[5], w[5], w[4]], axis=0),
+                NTD,
+                preferred_element_type=F32,
+            )
+            for x, w in zip(tends, made)
+        ]
+        splits = [reduce(x, w[3], w[1]) for x, w in zip(backs, made)]
+        outs = [
+            lax.dot_general(merge_ref[...], x, NTD, preferred_element_type=F32).astype(BF16)
+            for x in splits
+        ]
+        for seat, value in zip(seats, outs):
+            out_ref[seat] = value
         return carry
 
-    lax.fori_loop(0, block, one, 0, unroll=2)
+    lax.fori_loop(0, block // GROUP, several, 0)
 
 
 def cycle_trips(values, wave_ids, points, coef, flip, fields):

time: 251 us -> 187 us (0.75)
  Pallas kernels: 123 us -> 59.1 us
    pallas_call x1, Pallas kernels: 107 us -> 43 us  [cycle_trips(): pl.pallas_call(functools.partial(cycle_kernel, fields), name='cycles', ou...]
  transfers between devices with their start and end apart: 2 -> 2, of which waited for: 2 -> 2; matrix products, arithmetic and copies ran while one was open for 0% -> 1% of each run, Pallas kernels for 0% -> 0%
where the time goes in v2:
time: 187 us
  waiting for transfers between devices  62.4 us (33%)
  Pallas kernels  59.1 us (32%)
  blocking collectives  34.9 us (19%)
  between operations  13.6 us (7%)
  local copies, waits for them, and re-layouts  8.63 us (5%)
  starting transfers between devices  7.48 us (4%)
    pallas_call x1, Pallas kernels, cycle_trips(): pl.pallas_call(functools.partial(cycle_kernel, fields), name='cycles', ou...  43 us
    all_to_all x1, blocking collectives, on_device(): lax.all_to_all(leaving, 'wave', split_axis=0, concat_axis=0, tiled=True)  34.9 us
    all_gather x1, waiting for transfers between devices, on_device(): gathered = lax.all_gather(projected, 'lev', axis=0)  32.1 us
    all_to_all x1, waiting for transfers between devices, on_device(): lax.all_to_all(fourier, 'wave', split_axis=0, concat_axis=0, tiled=True)  30.3 us
    all_to_all x1, starting transfers between devices, on_device(): lax.all_to_all(fourier, 'wave', split_axis=0, concat_axis=0, tiled=True)  7.44 us
    unnamed x22, local copies, waits for them, and re-layouts  6.22 us
    pallas_call x1, Pallas kernels, vertical(): pl.pallas_call(body, name='vertical', out_shape=jax.ShapeDtypeStruct((wav...  6.21 us
    pallas_call x1, Pallas kernels, inverse_legendre(): pl.pallas_call(inverse_kernel, name='inverse', out_shape=jax.ShapeDtypeSt...  4.99 us
  transfers between devices with their start and end apart: 2, of which 2 were waited for; matrix products, arithmetic and copies ran while one was open for 1% of the time, Pallas kernels for 0%

profile of v2, /device:TPU:0, one launch (start us, length us, event | category | flops | bytes accessed | tf_op | source)
XLA Modules:
  0.0 186.9 jit_solution(6766238440462322670)
XLA Ops:
  6.5 0.0 copy-start
  6.5 0.7 dynamic_slice.13.lengths
  7.3 2.9 %copy-done.1 = bf16[4,640,1280]{2,1,0:T(8,128)(2,1)S(1)} copy-done((bf16[4,640,1280]{2,1,0:T(8,128)(2,1)S(1)}, bf16[4,640,1280]{2,1,0:T(8,128)(2,1)}, u32[]{:S(2)}) %copy-start.1) | copy-done | bytes 6553624
  10.1 1.2 copy-done.3
  11.3 5.0 %inverse.1 = bf16[8,4,160,96]{3,2,1,0:T(8,128)(2,1)} custom-call(s32[4]{0:T(128)S(1)} %dynamic_slice.13.lengths, bf16[4,6,16,1280]{3,2,1,0:T(8,128)(2,1)S(1)} %copy-done.3, bf16[4,640,1280]{2,1,0:T(8,128)(2,1)S(1)} %copy-done.1), custom_call_target="tpu_custom_call" | custom-call | flops 1258291200 | bytes 6553600 | tf_op jit(solution)/shard_map/inverse/pallas_call | solution.py:78
  16.3 7.4 %all-to-all-start = ((bf16[8,4,160,96]{3,2,1,0:T(8,128)(2,1)}), bf16[8,4,160,96]{3,2,1,0:T(8,128)(2,1)S(1)}, u32[]{:S(2)}, u32[]{:S(2)}) async-start(bf16[8,4,160,96]{3,2,1,0:T(8,128)(2,1)} %inverse.1), calls=%async_computation | async-start | bytes 2621440 | tf_op jit(solution)/shard_map/all_to_all | solution.py:382
  23.8 0.0 all-gather.3.cloned.1.call-start
  23.8 0.0 copy-done.8
  23.9 0.1 convert_element_type.46
  24.1 0.8 broadcast_divide_fusion
  24.9 0.0 copy-start.5
  24.9 30.3 %all-to-all-done = bf16[8,4,160,96]{3,2,1,0:T(8,128)(2,1)S(1)} async-done(((bf16[8,4,160,96]{3,2,1,0:T(8,128)(2,1)}), bf16[8,4,160,96]{3,2,1,0:T(8,128)(2,1)S(1)}, u32[]{:S(2)}, u32[]{:S(2)}) %all-to-all-start) | async-done | bytes 983072 | tf_op jit(solution)/shard_map/all_to_all | solution.py:382
  55.2 0.7 copy.13
  55.8 0.1 broadcast_in_dim.39.wave_ref
  55.9 0.0 copy-done.5
  55.9 43.0 %cycles.1 = bf16[160,32,96]{2,1,0:T(8,128)(2,1)S(1)} custom-call(s32[1]{0:T(128)} %bitcast.flip, f32[160]{0:T(256)S(1)} %get-tuple-element.6.points, f32[160]{0:T(256)S(1)} %get-tuple-element.5.inverses, bf16[160,32,96]{2,1,0:T(8,128)(2,1)S(1)} %bitcast.10, f32[160,2560]{1,0:T(8,128)S(1)} %copy-done.5, f32[8,128]{1,0:T(8,128)S(1)} %stack.5.lane_ref, ...), custom_call_target="tpu_custom_call" | custom-call | flops 5033164800 | bytes 1638400 | tf_op jit(solution)/shard_map/cycles/pallas_call | solution.py:278
  98.9 0.5 copy.14
  99.4 0.0 copy-start.6
  99.5 34.9 %all_to_all.10.values_ref = bf16[8,4,160,96]{3,2,1,0:T(8,128)(2,1)S(1)} all-to-all(bf16[8,4,160,96]{3,2,1,0:T(8,128)(2,1)S(1)} %bitcast.12), channel_id=1, replica_groups=mesh['wave'=8,'lev'=4] {'wave'}, dimensions={0} | all-to-all | bytes 1966080 | tf_op jit(solution)/shard_map/all_to_all | solution.py:388
  134.4 0.0 copy-done.6
  134.4 0.1 broadcast_in_dim.40.weight_ref
  134.6 0.0 slice-done
  134.6 0.0 copy-start.7
  134.6 0.0 copy-start.4
  134.6 4.9 %forward.1 = bf16[4,96,1280]{2,1,0:T(8,128)(2,1)} custom-call(s32[4]{0:T(128)S(1)} %dynamic_slice.13.lengths, bf16[8,4,160,96]{3,2,1,0:T(8,128)(2,1)S(1)} %all_to_all.10.values_ref, bf16[4,640,1280]{2,1,0:T(8,128)(2,1)S(1)} %bitcast.8, f32[640,128]{1,0:T(8,128)S(1)} %broadcast_in_dim.40.weight_ref), custom_call_target="tpu_custom_call" | custom-call | flops 1258291200 | bytes 6553600 | tf_op jit(solution)/shard_map/forward/pallas_call | solution.py:124
  139.5 0.0 all-gather.3.cloned.1.call-update
  139.5 0.1 dynamic_slice.12.ids
  139.6 0.0 copy-done
  139.6 32.1 %all-gather.3.cloned.1.call-done = bf16[16,96,1280]{2,1,0:T(8,128)(2,1)} async-done(((bf16[4,96,1280]{2,1,0:T(8,128)(2,1)}), bf16[16,96,1280]{2,1,0:T(8,128)(2,1)}) %all-gather.3.cloned.1.call-update) | async-done | bytes 3932176 | tf_op jit(solution)/shard_map/all_gather | solution.py:390
  171.7 0.1 broadcast_in_dim.41.depth_ref
  171.8 2.1 %copy-done.2 = bf16[16,96,1280]{2,1,0:T(8,128)(2,1)S(1)} copy-done((bf16[16,96,1280]{2,1,0:T(8,128)(2,1)S(1)}, bf16[16,96,1280]{2,1,0:T(8,128)(2,1)}, u32[]{:S(2)}) %copy-start.2) | copy-done | bytes 3932184
  173.9 6.2 %vertical.1 = bf16[4,6,16,1280]{3,2,1,0:T(8,128)(2,1)} custom-call(s32[4]{0:T(128)S(1)} %dynamic_slice.12.ids, bf16[4,4,96,1280]{3,2,1,0:T(8,128)(2,1)S(1)} %bitcast.9, bf16[64,64]{1,0:T(8,128)(2,1)S(1)} %copy-done.4, bf16[16,64]{1,0:T(8,128)(2,1)S(1)} %constant_dynamic-slice_fusion.own_ref, f32[64,128]{1,0:T(8,128)S(1)} %broadcast_in_dim.41.depth_ref), custom_call_target="tpu_custom_call" | custom-call | tf_op jit(solution)/shard_map/vertical/pallas_call | solution.py:342
  (23 shorter events, 0.1 us)
Async XLA Ops:
  6.5 133.1 %copy-start = (bf16[64,64]{1,0:T(8,128)(2,1)S(1)}, bf16[64,64]{1,0:T(8,128)(2,1)}, u32[]{:S(2)}) copy-start(bf16[64,64]{1,0:T(8,128)(2,1)} %param.18) | copy-start | bytes 24580
  7.3 2.9 %copy-start.1 = (bf16[4,640,1280]{2,1,0:T(8,128)(2,1)S(1)}, bf16[4,640,1280]{2,1,0:T(8,128)(2,1)}, u32[]{:S(2)}) copy-start(bf16[4,640,1280]{2,1,0:T(8,128)(2,1)} %leg_ref.3) | copy-start | bytes 19660804
  10.1 1.2 copy-start.3
  16.3 7.5 %copy-start.8 = (s32[32]{0:T(128)S(1)}, s32[32]{0:T(128)}, u32[]{:S(2)}) copy-start(s32[32]{0:T(128)} %param.12) | copy-start | bytes 388
  16.3 38.8 %all-to-all-start = ((bf16[8,4,160,96]{3,2,1,0:T(8,128)(2,1)}), bf16[8,4,160,96]{3,2,1,0:T(8,128)(2,1)S(1)}, u32[]{:S(2)}, u32[]{:S(2)}) async-start(bf16[8,4,160,96]{3,2,1,0:T(8,128)(2,1)} %inverse.1), calls=%async_computation | async-start | bytes 2621440 | tf_op jit(solution)/shard_map/all_to_all | solution.py:382
  23.8 147.9 %all-gather.3.cloned.1.call-start = ((), (), s32[]{:S(2)}) async-start(), calls=%async_computation.2 | async-start | bytes 4915200 | tf_op jit(solution)/shard_map/all_gather | solution.py:390
  24.9 31.1 %copy-start.5 = (f32[160,2560]{1,0:T(8,128)S(1)}, f32[160,2560]{1,0:T(8,128)}, u32[]{:S(2)}) copy-start(f32[160,2560]{1,0:T(8,128)} %coef_ref.1) | copy-start | bytes 4915204
  55.2 79.4 %slice-start = ((s8[6553600]{0:T(1024)(128)(4,1)}), s8[4194304]{0:T(1024)(128)(4,1)S(1)}, s32[]{:S(2)}) async-start(s8[6553600]{0:T(1024)(128)(4,1)} %bitcast.7), calls=%async_computation.3 | async-start | bytes 8388608
  55.9 78.7 %slice-start.1 = ((s8[6553600]{0:T(1024)(128)(4,1)}), s8[2359296]{0:T(1024)(128)(4,1)S(1)}, s32[]{:S(2)}) async-start(s8[6553600]{0:T(1024)(128)(4,1)} %bitcast.7), calls=%async_computation.4 | async-start | bytes 4718592
  99.4 35.0 %copy-start.6 = (f32[640]{0:T(1024)S(1)}, f32[640]{0:T(1024)}, u32[]{:S(2)}) copy-start(f32[640]{0:T(1024)} %param.16) | copy-start | bytes 7684
  134.6 37.1 %copy-start.7 = (f32[64]{0:T(128)S(1)}, f32[64]{0:T(128)}, u32[]{:S(2)}) copy-start(f32[64]{0:T(128)} %param.19) | copy-start | bytes 772
  134.6 37.2 %copy-start.4 = (bf16[64,64]{1,0:T(8,128)(2,1)S(1)}, bf16[64,64]{1,0:T(8,128)(2,1)}, u32[]{:S(2)}) copy-start(bf16[64,64]{1,0:T(8,128)(2,1)} %in_ref.1) | copy-start | bytes 24580
  171.8 2.1 %copy-start.2 = (bf16[16,96,1280]{2,1,0:T(8,128)(2,1)S(1)}, bf16[16,96,1280]{2,1,0:T(8,128)(2,1)}, u32[]{:S(2)}) copy-start(bf16[16,96,1280]{2,1,0:T(8,128)(2,1)} %all-gather.3.cloned.1.call-done) | copy-start | bytes 11796484
Sparse Core Ops, SparseCore 0:
  139.6 32.0 all-gather.2
